TPU v7x, 32 devices: a whole 2x2x4 slice. The times are simulated.
32 devices in a mesh: img: 8 (over z, x), row: 4 (over y, core).
Axes of the slice: x: 2, y: 2, z: 4, core: 2. Of those that a mesh axis runs over, the one named last changes fastest.
Arguments:
- tokens: bfloat16 [8, 32, 128, 1024], P('img', 'row'), may hold values from -14 to 14
- proj_weight: bfloat16 [1024, 256], replicated, may hold values from -0.1875 to 0.1875
- proj_bias: float32 [256], replicated, may hold values from -3 to 3
- conv_weight: bfloat16 [4, 3, 3, 256, 256], replicated, may hold values from -0.125 to 0.125
- bn_gain: float32 [4, 256], replicated, may hold values from 0.1 to 1.9
- bn_bias: float32 [4, 256], replicated, may hold values from -3 to 3
Outputs:
- joining_out: bfloat16 [8, 32, 128, 256], P('img', 'row')
All inputs are finite; a program needn't handle non-finite values.
Results may differ from a plain program's by a relative error of at most 0.0071.
Values may be sent and summed in bfloat16 or wider, within the bound.
A program may use at most 64 MiB of HBM per device.

v0:
```python
import jax
import jax.numpy as jnp
from jax import lax
from jax.sharding import PartitionSpec as P

epsilon = 1e-05


def extended(value, sides, width):
    for axis, dim in sides:
        devices, length = (lax.axis_size(axis), value.shape[dim])
        up = [(i, (i + 1) % devices) for i in range(devices - 1)]
        down = [(j, i) for i, j in up]
        last = lax.slice_in_dim(value, length - width, length, axis=dim)
        leading = lax.slice_in_dim(value, 0, width, axis=dim)
        before = lax.ppermute(last, axis, up)
        after = lax.ppermute(leading, axis, down)
        value = jnp.concatenate([before, value, after], axis=dim)
    return value


def conv_valid(padded, kernel):
    return lax.conv_general_dilated(
        padded,
        kernel,
        (1, 1),
        ((0, 0), (1, 1)),
        dimension_numbers=("NHWC", "HWIO", "NHWC"),
        preferred_element_type=jnp.float32,
    )


def batch_norm(conv_out, interior, gain_row, shift_row, cell_total):
    first_moment, squares = lax.psum(
        (jnp.sum(interior, axis=(0, 1, 2)), jnp.sum(jnp.square(interior), axis=(0, 1, 2))),
        ("img", "row"),
    )
    average = first_moment / cell_total
    spread = squares / cell_total - average * average
    return (conv_out - average) * lax.rsqrt(spread + epsilon) * gain_row + shift_row


def rim_conv(source, kernel):
    padded = extended(source, (("row", 1),), 1)
    return conv_valid(padded, kernel)


def residual_unit(source, conv_weight, bn_gain, bn_bias, first, cell_total):
    conv_first = rim_conv(jax.nn.relu(source), conv_weight[first])
    hidden = jax.nn.relu(
        batch_norm(conv_first, conv_first, bn_gain[first], bn_bias[first], cell_total)
    ).astype(jnp.bfloat16)
    conv_second = rim_conv(hidden, conv_weight[first + 1])
    branch = batch_norm(
        conv_second, conv_second, bn_gain[first + 1], bn_bias[first + 1], cell_total
    )
    return source.astype(jnp.float32) + branch


def on_device(tokens, proj_weight, proj_bias, conv_weight, bn_gain, bn_bias):
    img_count, row_count, col_count, embed_dim = tokens.shape
    flat = (
        jnp.dot(tokens.reshape(-1, embed_dim), proj_weight, preferred_element_type=jnp.float32)
        + proj_bias
    )
    feature = flat.astype(jnp.bfloat16).reshape(img_count, row_count, col_count, -1)
    cell_total = float(
        lax.axis_size("img") * lax.axis_size("row") * img_count * row_count * col_count
    )
    joined = residual_unit(feature, conv_weight, bn_gain, bn_bias, 0, cell_total).astype(
        jnp.bfloat16
    )
    return residual_unit(joined, conv_weight, bn_gain, bn_bias, 2, cell_total).astype(jnp.bfloat16)


def solution(mesh):
    in_specs = (P("img", "row", None, None), P(), P(), P(), P(), P())
    out_specs = P("img", "row", None, None)
    return jax.shard_map(
        on_device, mesh=mesh, in_specs=in_specs, out_specs=out_specs, check_vma=False
    )
```

profile of v0, /device:TPU:0, one launch (start us, length us, event | category | flops | bytes accessed | tf_op | source)
XLA Modules:
  0.0 233.8 jit_solution(10061670409957228319)
XLA Ops:
  0.0 0.0 copy-start
  0.0 1.6 copy-done
  1.6 1.8 broadcast_maximum_fusion.1
  3.4 2.4 %collective-permute-start = (bf16[1,1,128,256]{3,2,1,0:T(8,128)(2,1)S(1)}, bf16[1,1,128,256]{3,2,1,0:T(8,128)(2,1)S(1)}, u32[]{:S(2)}, u32[]{:S(2)}) collective-permute-start(bf16[1,1,128,256]{3,2,1,0:T(8,128)(2,1)S(1)} %get-tuple-element.29), channel_id=1, source_target_pairs={{0,1},{1,2},{2,3},{4,5},{5,6},{6,7},{8,9},{9,10},{10,11},{12,13},{... | collective-permute-start | bytes 196616 | tf_op jit(solution)/shard_map/ppermute | solution.py:16
  5.8 1.3 collective-permute-start.1
  7.1 0.0 copy-done.4
  7.2 0.1 convert.1
  7.3 0.0 collective-permute-done
  7.3 3.8 %collective-permute-done.1 = bf16[1,1,128,256]{3,2,1,0:T(8,128)(2,1)S(1)} collective-permute-done((bf16[1,1,128,256]{3,2,1,0:T(8,128)(2,1)S(1)}, bf16[1,1,128,256]{3,2,1,0:T(8,128)(2,1)S(1)}, u32[]{:S(2)}, u32[]{:S(2)}) %collective-permute-start.1) | collective-permute-done | bytes 65568 | tf_op jit(solution)/shard_map/ppermute | solution.py:17
  11.1 0.1 maximum_bitcast_fusion.3
  11.2 1.0 pad
  12.2 2.2 reshape.84
  14.4 1.4 copy.8
  15.8 3.7 %select_reduce_fusion.7 = (f32[256]{0:T(256)S(1)}, f32[256]{0:T(256)S(1)}, f32[8,8,17,256]{3,1,2,0:T(8,128)}) fusion(pred[8,17]{0,1:T(8,128)(4,1)S(1)} %copy-done.5, bf16[4,3,3,256,256]{4,3,2,1,0:T(8,128)(2,1)} %param.9, bf16[10,1,7,2,256]{4,2,3,0,1:T(8,128)(2,1)S(1)} %slice.98, bf16[10,1,8,17,256]{4,2,3,0,1:T(8,128)(2,1)S(1)} %copy.8), kind=kOutput, calls=%fused_computation.30 | convolution fusion | flops 1287462400 | bytes 3063944 | tf_op jit(solution)/shard_map/conv_general_dilated | solution.py:23
  19.5 41.9 %all-reduce.3 = (f32[256]{0:T(256)S(1)}, f32[256]{0:T(256)S(1)}) all-reduce(f32[256]{0:T(256)S(1)} %get-tuple-element.12, f32[256]{0:T(256)S(1)} %get-tuple-element.11), channel_id=1, replica_groups=mesh['img'=8,'row'=4] {'img','row'}, use_global_device_ids=true, to_apply=%region_3.4 | all-reduce | flops 512 | bytes 4096 | tf_op jit(solution)/shard_map/psum | solution.py:34
  61.4 1.5 maximum_convert_fusion.1
  62.9 0.9 copy.10
  63.8 0.6 slice.100
  64.5 1.3 collective-permute-start.2
  65.8 0.1 reshape.155
  65.8 0.1 slice.103
  66.0 1.3 collective-permute-start.3
  67.3 1.1 slice_bitcast_fusion.3
  68.3 0.0 collective-permute-done.2
  68.4 0.1 copy.13
  68.5 3.2 %collective-permute-done.3 = bf16[1,1,128,256]{3,1,2,0:T(2,128)(2,1)S(1)} collective-permute-done((bf16[1,1,128,256]{3,1,2,0:T(2,128)(2,1)S(1)}, bf16[1,1,128,256]{3,1,2,0:T(2,128)(2,1)S(1)}, u32[]{:S(2)}, u32[]{:S(2)}) %collective-permute-start.3) | collective-permute-done | bytes 65568 | tf_op jit(solution)/shard_map/ppermute | solution.py:17
  71.7 0.7 maximum_bitcast_fusion
  72.4 0.1 pad.2
  72.6 0.2 copy.16
  72.8 3.7 %select_reduce_fusion.5 = (f32[256]{0:T(256)S(1)}, f32[256]{0:T(256)S(1)}, f32[8,8,17,256]{3,1,2,0:T(8,128)}) fusion(pred[8,17]{0,1:T(8,128)(4,1)S(1)} %copy-done.5, bf16[4,3,3,256,256]{4,3,2,1,0:T(8,128)(2,1)} %param.9, bf16[10,1,7,2,256]{4,2,3,0,1:T(8,128)(2,1)S(1)} %slice.104, bf16[10,1,8,17,256]{4,2,3,0,1:T(8,128)(2,1)S(1)} %copy.16), kind=kOutput, calls=%fused_computation.27 | convolution fusion | flops 1287462400 | bytes 3063944 | tf_op jit(solution)/shard_map/conv_general_dilated | solution.py:23
  76.5 41.3 %all-reduce.2 = (f32[256]{0:T(256)S(1)}, f32[256]{0:T(256)S(1)}) all-reduce(f32[256]{0:T(256)S(1)} %get-tuple-element.10, f32[256]{0:T(256)S(1)} %get-tuple-element.9), channel_id=1, replica_groups=mesh['img'=8,'row'=4] {'img','row'}, use_global_device_ids=true, to_apply=%region_7.8 | all-reduce | flops 512 | bytes 4096 | tf_op jit(solution)/shard_map/psum | solution.py:34
  117.8 1.4 multiply_add_fusion.1
  119.2 0.4 copy.17
  119.6 1.5 broadcast_maximum_fusion
  121.1 0.2 fusion.60
  121.2 1.3 collective-permute-start.4
  122.6 1.5 collective-permute-start.5
  124.0 0.0 collective-permute-done.4
  124.0 4.2 %collective-permute-done.5 = bf16[1,1,128,256]{3,1,2,0:T(2,128)(2,1)S(1)} collective-permute-done((bf16[1,1,128,256]{3,1,2,0:T(2,128)(2,1)S(1)}, bf16[1,1,128,256]{3,1,2,0:T(2,128)(2,1)S(1)}, u32[]{:S(2)}, u32[]{:S(2)}) %collective-permute-start.5) | collective-permute-done | bytes 65568 | tf_op jit(solution)/shard_map/ppermute | solution.py:17
  128.3 0.7 maximum_bitcast_fusion.1
  129.0 0.1 pad.4
  129.1 0.2 copy.21
  129.4 3.7 %select_reduce_fusion.3 = (f32[256]{0:T(256)S(1)}, f32[256]{0:T(256)S(1)}, f32[8,8,17,256]{3,1,2,0:T(8,128)}) fusion(pred[8,17]{0,1:T(8,128)(4,1)S(1)} %copy-done.5, bf16[4,3,3,256,256]{4,3,2,1,0:T(8,128)(2,1)} %param.9, bf16[10,1,7,2,256]{4,2,3,0,1:T(8,128)(2,1)S(1)} %slice.108, bf16[10,1,8,17,256]{4,2,3,0,1:T(8,128)(2,1)S(1)} %copy.21), kind=kOutput, calls=%fused_computation.24 | convolution fusion | flops 1287462400 | bytes 3063944 | tf_op jit(solution)/shard_map/conv_general_dilated | solution.py:23
  133.1 41.1 %all-reduce.1 = (f32[256]{0:T(256)S(1)}, f32[256]{0:T(256)S(1)}) all-reduce(f32[256]{0:T(256)S(1)} %get-tuple-element.8, f32[256]{0:T(256)S(1)} %get-tuple-element.7), channel_id=1, replica_groups=mesh['img'=8,'row'=4] {'img','row'}, use_global_device_ids=true, to_apply=%region_11.12 | all-reduce | flops 512 | bytes 4096 | tf_op jit(solution)/shard_map/psum | solution.py:34
  174.3 1.5 maximum_convert_fusion
  175.8 0.9 copy.23
  176.7 1.4 collective-permute-start.6
  178.2 0.1 reshape.156
  178.3 0.1 slice.113
  178.4 1.3 collective-permute-start.7
  179.8 0.0 collective-permute-done.6
  179.8 0.1 copy.26
  179.9 4.3 %collective-permute-done.7 = bf16[1,1,128,256]{3,1,2,0:T(2,128)(2,1)S(1)} collective-permute-done((bf16[1,1,128,256]{3,1,2,0:T(2,128)(2,1)S(1)}, bf16[1,1,128,256]{3,1,2,0:T(2,128)(2,1)S(1)}, u32[]{:S(2)}, u32[]{:S(2)}) %collective-permute-start.7) | collective-permute-done | bytes 65568 | tf_op jit(solution)/shard_map/ppermute | solution.py:17
  184.2 0.7 maximum_bitcast_fusion.2
  184.9 0.1 pad.6
  185.0 0.2 copy.29
  185.2 3.7 %select_reduce_fusion.1 = (f32[256]{0:T(256)S(1)}, f32[256]{0:T(256)S(1)}, f32[8,8,17,256]{3,1,2,0:T(8,128)}) fusion(pred[8,17]{0,1:T(8,128)(4,1)S(1)} %copy-done.5, bf16[4,3,3,256,256]{4,3,2,1,0:T(8,128)(2,1)} %param.9, bf16[10,1,7,2,256]{4,2,3,0,1:T(8,128)(2,1)S(1)} %slice.114, bf16[10,1,8,17,256]{4,2,3,0,1:T(8,128)(2,1)S(1)} %copy.29), kind=kOutput, calls=%fused_computation.21 | convolution fusion | flops 1287462400 | bytes 3063944 | tf_op jit(solution)/shard_map/conv_general_dilated | solution.py:23
  189.0 41.4 %all-reduce = (f32[256]{0:T(256)S(1)}, f32[256]{0:T(256)S(1)}) all-reduce(f32[256]{0:T(256)S(1)} %get-tuple-element.6, f32[256]{0:T(256)S(1)} %get-tuple-element.5), channel_id=1, replica_groups=mesh['img'=8,'row'=4] {'img','row'}, use_global_device_ids=true, to_apply=%region_15.16 | all-reduce | flops 512 | bytes 4096 | tf_op jit(solution)/shard_map/psum | solution.py:34
  230.3 1.4 multiply_add_fusion
  231.8 0.0 copy-start.2
  231.8 0.4 copy.30
  232.1 0.7 copy-done.2
  232.8 0.1 fusion.14
  232.9 0.9 copy.31
  (28 shorter events, 0.4 us)
Async XLA Ops:
  0.0 1.6 copy-start
  1.6 5.5 %copy-start.3 = (f32[4,256]{1,0:T(4,128)S(1)}, f32[4,256]{1,0:T(4,128)}, u32[]{:S(2)}) copy-start(f32[4,256]{1,0:T(4,128)} %param.10) | copy-start | bytes 12292
  1.6 5.5 %copy-start.4 = (f32[4,256]{1,0:T(4,128)S(1)}, f32[4,256]{1,0:T(4,128)}, u32[]{:S(2)}) copy-start(f32[4,256]{1,0:T(4,128)} %param.11) | copy-start | bytes 12292
  3.4 3.9 %collective-permute-start = (bf16[1,1,128,256]{3,2,1,0:T(8,128)(2,1)S(1)}, bf16[1,1,128,256]{3,2,1,0:T(8,128)(2,1)S(1)}, u32[]{:S(2)}, u32[]{:S(2)}) collective-permute-start(bf16[1,1,128,256]{3,2,1,0:T(8,128)(2,1)S(1)} %get-tuple-element.29), channel_id=1, source_target_pairs={{0,1},{1,2},{2,3},{4,5},{5,6},{6,7},{8,9},{9,10},{10,11},{12,13},{... | collective-permute-start | bytes 196616 | tf_op jit(solution)/shard_map/ppermute | solution.py:16
  5.8 5.3 %collective-permute-start.1 = (bf16[1,1,128,256]{3,2,1,0:T(8,128)(2,1)S(1)}, bf16[1,1,128,256]{3,2,1,0:T(8,128)(2,1)S(1)}, u32[]{:S(2)}, u32[]{:S(2)}) collective-permute-start(bf16[1,1,128,256]{3,2,1,0:T(8,128)(2,1)S(1)} %get-tuple-element.30), channel_id=1, source_target_pairs={{1,0},{2,1},{3,2},{5,4},{6,5},{7,6},{9,8},{10,9},{11,10},{13,12},{... | collective-permute-start | bytes 196616 | tf_op jit(solution)/shard_map/ppermute | solution.py:17
  14.4 1.4 copy-start.5
  64.5 3.9 %collective-permute-start.2 = (bf16[1,1,128,256]{3,2,1,0:T(8,128)(2,1)}, bf16[1,1,128,256]{3,2,1,0:T(8,128)(2,1)S(1)}, u32[]{:S(2)}, u32[]{:S(2)}) collective-permute-start(bf16[1,1,128,256]{3,2,1,0:T(8,128)(2,1)} %slice.100), channel_id=1, source_target_pairs={{0,1},{1,2},{2,3},{4,5},{5,6},{6,7},{8,9},{9,10},{10,11},{12,13},{... | collective-permute-start | bytes 196616 | tf_op jit(solution)/shard_map/ppermute | solution.py:16
  66.0 5.7 %collective-permute-start.3 = (bf16[1,1,128,256]{3,1,2,0:T(2,128)(2,1)S(1)}, bf16[1,1,128,256]{3,1,2,0:T(2,128)(2,1)S(1)}, u32[]{:S(2)}, u32[]{:S(2)}) collective-permute-start(bf16[1,1,128,256]{3,1,2,0:T(2,128)(2,1)S(1)} %slice.103), channel_id=1, source_target_pairs={{1,0},{2,1},{3,2},{5,4},{6,5},{7,6},{9,8},{10,9},{11,10},{13,12},{... | collective-permute-start | bytes 196616 | tf_op jit(solution)/shard_map/ppermute | solution.py:17
  121.2 2.8 %collective-permute-start.4 = (bf16[1,1,128,256]{3,1,2,0:T(2,128)(2,1)S(1)}, bf16[1,1,128,256]{3,1,2,0:T(2,128)(2,1)S(1)}, u32[]{:S(2)}, u32[]{:S(2)}) collective-permute-start(bf16[1,1,128,256]{3,1,2,0:T(2,128)(2,1)S(1)} %get-tuple-element.27), channel_id=1, source_target_pairs={{0,1},{1,2},{2,3},{4,5},{5,6},{6,7},{8,9},{9,10},{10,11},{12,13},{... | collective-permute-start | bytes 196616 | tf_op jit(solution)/shard_map/ppermute | solution.py:16
  122.6 5.7 %collective-permute-start.5 = (bf16[1,1,128,256]{3,1,2,0:T(2,128)(2,1)S(1)}, bf16[1,1,128,256]{3,1,2,0:T(2,128)(2,1)S(1)}, u32[]{:S(2)}, u32[]{:S(2)}) collective-permute-start(bf16[1,1,128,256]{3,1,2,0:T(2,128)(2,1)S(1)} %get-tuple-element.28), channel_id=1, source_target_pairs={{1,0},{2,1},{3,2},{5,4},{6,5},{7,6},{9,8},{10,9},{11,10},{13,12},{... | collective-permute-start | bytes 196616 | tf_op jit(solution)/shard_map/ppermute | solution.py:17
  176.7 3.0 %copy-start.1 = (bf16[8,8,17,256]{3,0,2,1:T(8,128)(2,1)S(1)}, bf16[8,8,17,256]{3,0,2,1:T(8,128)(2,1)}, u32[]{:S(2)}) copy-start(bf16[8,8,17,256]{3,0,2,1:T(8,128)(2,1)} %copy.23) | copy-start | bytes 1671172
  176.7 3.0 %collective-permute-start.6 = (bf16[1,1,128,256]{3,2,1,0:T(8,128)(2,1)S(1)}, bf16[1,1,128,256]{3,2,1,0:T(8,128)(2,1)S(1)}, u32[]{:S(2)}, u32[]{:S(2)}) collective-permute-start(bf16[1,1,128,256]{3,2,1,0:T(8,128)(2,1)S(1)} %slice.110), channel_id=1, source_target_pairs={{0,1},{1,2},{2,3},{4,5},{5,6},{6,7},{8,9},{9,10},{10,11},{12,13},{... | collective-permute-start | bytes 196616 | tf_op jit(solution)/shard_map/ppermute | solution.py:16
  178.4 5.7 %collective-permute-start.7 = (bf16[1,1,128,256]{3,1,2,0:T(2,128)(2,1)S(1)}, bf16[1,1,128,256]{3,1,2,0:T(2,128)(2,1)S(1)}, u32[]{:S(2)}, u32[]{:S(2)}) collective-permute-start(bf16[1,1,128,256]{3,1,2,0:T(2,128)(2,1)S(1)} %slice.113), channel_id=1, source_target_pairs={{1,0},{2,1},{3,2},{5,4},{6,5},{7,6},{9,8},{10,9},{11,10},{13,12},{... | collective-permute-start | bytes 196616 | tf_op jit(solution)/shard_map/ppermute | solution.py:17
  231.8 1.0 copy-start.2
where the time goes:
time: 235 us; the launch traced here: 234 us
  blocking collectives  166 us (71%)
  matrix products  16.7 us (7%)
  waiting for transfers between devices  15.6 us (7%)
  local copies, waits for them, and re-layouts  14.1 us (6%)
  starting transfers between devices  11.8 us (5%)
  other arithmetic  9.63 us (4%)
    psum x4, blocking collectives, batch_norm(): lax.psum((jnp.sum(interior, axis=(0, 1, 2)), jnp.sum(jnp.square(interior)...  166 us
    ppermute x4, waiting for transfers between devices, extended(): after = lax.ppermute(leading, axis, down)  15.6 us
    conv_general_dilated x4, matrix products, conv_valid(): lax.conv_general_dilated(padded, kernel, (1, 1), ((0, 0), (1, 1)), dimens...  15 us
    ppermute x4, starting transfers between devices, extended(): before = lax.ppermute(last, axis, up)  6.4 us
    ppermute x4, starting transfers between devices, extended(): after = lax.ppermute(leading, axis, down)  5.35 us
  transfers between devices with their start and end apart: 8, of which 4 were waited for; matrix products, arithmetic and copies ran while one was open for 1% of the time, Pallas kernels for 0%

commit v1 on v0

v1 whole, which is shorter than its diff:
```python
import functools

import jax
import jax.numpy as jnp
from jax import lax
from jax.experimental import pallas as pl
from jax.experimental.pallas import tpu as pltpu
from jax.sharding import PartitionSpec as P

epsilon = 1e-05
MESH = pl.DeviceIdType.MESH
F32 = jnp.float32
BF16 = jnp.bfloat16


def kernel(
    imgs,
    strips,
    height,
    cols,
    tokens_ref,
    pw_ref,
    pb_ref,
    cw_ref,
    gain_ref,
    bias_ref,
    out_ref,
    tok,
    pw,
    cw,
    feat,
    joined,
    xcat,
    raw,
    stat,
    peers,
    load_sem,
    weight_sem,
    halo_send,
    halo_recv,
    stat_send,
    stat_recv,
):
    count = imgs * strips
    width = feat.shape[-1]
    cells = height * cols
    me_img, me_row = lax.axis_index("img"), lax.axis_index("row")
    me = me_img * strips + me_row
    has_up, has_down = me_row > 0, me_row < strips - 1

    def peer(distance):
        target = lax.rem(me + distance, count)
        return {"img": target // strips, "row": lax.rem(target, strips)}

    def rows(first, number):
        return pl.ds(first * cols, number * cols)

    loads = [
        pltpu.make_async_copy(pw_ref, pw, load_sem.at[0]),
        pltpu.make_async_copy(tokens_ref.at[rows(0, 1)], tok.at[rows(0, 1)], load_sem.at[1]),
        pltpu.make_async_copy(
            tokens_ref.at[rows(height - 1, 1)], tok.at[rows(height - 1, 1)], load_sem.at[2]
        ),
        pltpu.make_async_copy(
            tokens_ref.at[rows(1, height - 2)], tok.at[rows(1, height - 2)], load_sem.at[3]
        ),
    ]
    weights = [
        pltpu.make_async_copy(
            cw_ref.at[pl.ds(3 * k, 3)], cw.at[pl.ds(3 * k, 3)], weight_sem.at[k]
        )
        for k in range(4)
    ]
    for load in loads:
        load.start()
    weights[0].start()

    barrier = pltpu.get_barrier_semaphore()

    @pl.loop(1, count)
    def _(distance):
        pl.semaphore_signal(barrier, inc=1, device_id=peer(distance), device_id_type=MESH)

    for k in range(1, 4):
        weights[k].start()

    @pl.when(jnp.logical_not(has_up))
    def _():
        xcat[rows(0, 1), :] = jnp.zeros((cols, 3 * width), BF16)

    @pl.when(jnp.logical_not(has_down))
    def _():
        xcat[rows(height + 1, 1), :] = jnp.zeros((cols, 3 * width), BF16)

    column = lax.broadcasted_iota(jnp.int32, (cols, width), 0)

    def span(row):
        return pl.ds(pl.multiple_of(row * cols, cols), cols)

    def put(row, value):
        at = span(row)
        xcat[at, 0:width] = jnp.where(column == 0, 0.0, pltpu.roll(value, 1, 0)).astype(BF16)
        xcat[at, width : 2 * width] = value.astype(BF16)
        xcat[at, 2 * width : 3 * width] = jnp.where(
            column == cols - 1, 0.0, pltpu.roll(value, cols - 1, 0)
        ).astype(BF16)

    def project(row):
        value = jnp.dot(tok[span(row), :], pw[...], preferred_element_type=F32) + pb_ref[...]
        value = value.astype(BF16)
        feat[span(row + 1), :] = value
        put(row + 1, jnp.maximum(value.astype(F32), 0.0))

    def halo(ref, phase):
        up = pltpu.make_async_remote_copy(
            src_ref=ref.at[rows(1, 1)],
            dst_ref=ref.at[rows(height + 1, 1)],
            send_sem=halo_send.at[phase, 0],
            recv_sem=halo_recv.at[phase, 1],
            device_id={"img": me_img, "row": jnp.maximum(me_row - 1, 0)},
            device_id_type=MESH,
        )
        down = pltpu.make_async_remote_copy(
            src_ref=ref.at[rows(height, 1)],
            dst_ref=ref.at[rows(0, 1)],
            send_sem=halo_send.at[phase, 1],
            recv_sem=halo_recv.at[phase, 0],
            device_id={"img": me_img, "row": jnp.minimum(me_row + 1, strips - 1)},
            device_id_type=MESH,
        )
        return up, down

    def send_halo(ref, phase):
        up, down = halo(ref, phase)

        @pl.when(has_up)
        def _():
            up.start()

        @pl.when(has_down)
        def _():
            down.start()

    def take_halo(ref, phase, top, bottom):
        up, down = halo(ref, phase)

        @pl.when(has_up)
        def _():
            down.wait_recv()
            top()

        @pl.when(has_down)
        def _():
            up.wait_recv()
            bottom()

    def end_halo(ref, phase):
        up, down = halo(ref, phase)

        @pl.when(has_up)
        def _():
            up.wait_send()

        @pl.when(has_down)
        def _():
            down.wait_send()

    def conv(k, first, number):
        total = None
        for dy in range(3):
            part = jnp.dot(
                xcat[rows(first + dy, number), :], cw[3 * k + dy], preferred_element_type=F32
            )
            total = part if total is None else total + part
        raw[k, rows(first + 1, number), :] = total
        return jnp.sum(total, axis=0, keepdims=True)

    def stat_copy(k, distance):
        return pltpu.make_async_remote_copy(
            src_ref=stat.at[k],
            dst_ref=peers.at[k, distance - 1],
            send_sem=stat_send.at[k],
            recv_sem=stat_recv.at[k],
            device_id=peer(distance),
            device_id_type=MESH,
        )

    def send_stat(k, sums):
        centre = sums / cells

        def add_row(row, squares):
            return squares + jnp.sum(
                jnp.square(raw[k, span(row + 1), :] - centre), axis=0, keepdims=True
            )

        squares = lax.fori_loop(0, height, add_row, jnp.zeros((1, width), F32))
        stat[k] = jnp.concatenate([sums, squares], axis=0)

        @pl.loop(1, count)
        def _(distance):
            stat_copy(k, distance).start()

    def take_stat(k):
        pltpu.make_async_copy(peers.at[k], peers.at[k], stat_recv.at[k]).wait()
        own = stat[k]
        every = peers[k]
        total = jnp.sum(every, axis=0) + own
        average = total[0:1] / (count * cells)
        gaps = jnp.sum(jnp.square(every[:, 0, :] - cells * average), axis=0, keepdims=True)
        gaps += jnp.square(own[0:1] - cells * average)
        spread = (total[1:2] + gaps / cells) / (count * cells)
        scale = lax.rsqrt(spread + epsilon) * gain_ref[pl.ds(k, 1), :]
        return average, scale, bias_ref[pl.ds(k, 1), :]

    def normed(k, row, norm):
        average, scale, shift = norm
        return (raw[k, span(row), :] - average) * scale + shift

    rim_first = [(0, 2), (height - 2, 2)]
    middle = [(first, 2) for first in range(2, height - 2, 2)]

    loads[0].wait()
    loads[1].wait()
    project(0)
    loads[2].wait()
    project(height - 1)
    pl.semaphore_wait(barrier, count - 1)
    send_halo(feat, 0)
    loads[3].wait()

    @pl.loop(1, height - 1)
    def _(row):
        project(row)

    def feature_rim(row):
        put(row, jnp.maximum(feat[span(row), :].astype(F32), 0.0))

    weights[0].wait()
    sums = sum(conv(0, first, number) for first, number in middle)
    take_halo(feat, 0, lambda: feature_rim(0), lambda: feature_rim(height + 1))
    sums += sum(conv(0, first, number) for first, number in rim_first)
    send_halo(raw.at[0], 1)
    send_stat(0, sums)

    def later_conv(k):
        weights[k].wait()
        sums = sum(conv(k, first, number) for first, number in rim_first)
        if k < 3:
            send_halo(raw.at[k], k + 1)
        sums += sum(conv(k, first, number) for first, number in middle)
        send_stat(k, sums)

    def hidden(k):
        norm = take_stat(k)

        def one(row):
            put(row, jnp.maximum(normed(k, row, norm), 0.0))

        pl.loop(1, height + 1)(one)
        take_halo(raw.at[k], k + 1, lambda: one(0), lambda: one(height + 1))

    hidden(0)
    later_conv(1)

    norm_1 = take_stat(1)

    def join(row, local):
        value = (feat[span(row), :].astype(F32) + normed(1, row, norm_1)).astype(BF16)
        if local:
            joined[span(row - 1), :] = value
        put(row, jnp.maximum(value.astype(F32), 0.0))

    pl.loop(1, height + 1)(lambda row: join(row, True))
    take_halo(raw.at[1], 2, lambda: join(0, False), lambda: join(height + 1, False))
    later_conv(2)
    hidden(2)
    later_conv(3)
    norm_3 = take_stat(3)

    @pl.loop(0, height)
    def _(row):
        value = joined[span(row), :].astype(F32) + normed(3, row + 1, norm_3)
        out_ref[span(row), :] = value.astype(BF16)

    end_halo(feat, 0)
    for k in range(3):
        end_halo(raw.at[k], k + 1)
    for k in range(4):
        pltpu.make_async_copy(peers.at[k], peers.at[k], stat_send.at[k]).wait()


def solution(mesh):
    imgs, strips = mesh.shape["img"], mesh.shape["row"]

    def on_device(tokens, proj_weight, proj_bias, conv_weight, bn_gain, bn_bias):
        images, height, cols, embed = tokens.shape
        convs, taps, _, width, _ = conv_weight.shape
        assert images == 1 and height % 2 == 0 and height >= 4
        count = imgs * strips
        cells = height * cols
        any_space = pl.BlockSpec(memory_space=pl.ANY)
        vmem = pl.BlockSpec(memory_space=pltpu.VMEM)
        out = pl.pallas_call(
            functools.partial(kernel, imgs, strips, height, cols),
            out_shape=jax.ShapeDtypeStruct((cells, width), BF16),
            in_specs=[any_space, any_space, vmem, any_space, vmem, vmem],
            out_specs=vmem,
            scratch_shapes=[
                pltpu.VMEM((cells, embed), BF16),
                pltpu.VMEM((embed, width), BF16),
                pltpu.VMEM((convs * taps, taps * width, width), BF16),
                pltpu.VMEM((cells + 2 * cols, width), BF16),
                pltpu.VMEM((cells, width), BF16),
                pltpu.VMEM((cells + 2 * cols, taps * width), BF16),
                pltpu.VMEM((convs, cells + 2 * cols, width), F32),
                pltpu.VMEM((convs, 2, width), F32),
                pltpu.VMEM((convs, count - 1, 2, width), F32),
                pltpu.SemaphoreType.DMA((4,)),
                pltpu.SemaphoreType.DMA((convs,)),
                pltpu.SemaphoreType.DMA((convs, 2)),
                pltpu.SemaphoreType.DMA((convs, 2)),
                pltpu.SemaphoreType.DMA((convs,)),
                pltpu.SemaphoreType.DMA((convs,)),
            ],
            compiler_params=pltpu.CompilerParams(
                collective_id=0, has_side_effects=True, vmem_limit_bytes=48 * 1024 * 1024
            ),
        )(
            tokens.reshape(cells, embed),
            proj_weight,
            proj_bias.reshape(1, width),
            conv_weight.reshape(convs * taps, taps * width, width),
            bn_gain,
            bn_bias,
        )
        return out.reshape(images, height, cols, width)

    in_specs = (P("img", "row", None, None), P(), P(), P(), P(), P())
    return jax.shard_map(
        on_device,
        mesh=mesh,
        in_specs=in_specs,
        out_specs=P("img", "row", None, None),
        check_vma=False,
    )
```

time: 235 us -> 42.6 us (0.18)
  blocking collectives: 166 us -> 0 us
  Pallas kernels: 0 us -> 36.9 us
  matrix products: 16.7 us -> 0 us
  waiting for transfers between devices: 15.6 us -> 0 us
  starting transfers between devices: 11.8 us -> 0 us
  other arithmetic: 9.63 us -> 0 us
  local copies, waits for them, and re-layouts: 14.1 us -> 5.48 us
    psum x4 -> x0, blocking collectives: 166 us -> none  [batch_norm(): lax.psum((jnp.sum(interior, axis=(0, 1, 2)), jnp.sum(jnp.square(interior)...]
    pallas_call x0 -> x1, Pallas kernels: none -> 36.9 us  [on_device(): pl.pallas_call(functools.partial(kernel, imgs, strips, height, cols), out...]
    ppermute x8 -> x0, waiting for transfers between devices: 15.6 us -> none  [the longest x4 15.6 us: extended(): after = lax.ppermute(leading, axis, down)]
    conv_general_dilated x4 -> x0, matrix products: 15 us -> none  [conv_valid(): lax.conv_general_dilated(padded, kernel, (1, 1), ((0, 0), (1, 1)), dimens...]
    ppermute x8 -> x0, starting transfers between devices: 11.8 us -> none  [the longest x4 6.4 us: extended(): before = lax.ppermute(last, axis, up)]
    convert_element_type x19 -> x0, local copies, waits for them, and re-layouts: 5 us -> none  [the longest x18 4.1 us: residual_unit(): hidden = jax.nn.relu(batch_norm(conv_first, conv_first, bn_gain[first], b...]
    conv_general_dilated x9 -> x0, local copies, waits for them, and re-layouts: 4.28 us -> none  [conv_valid(): lax.conv_general_dilated(padded, kernel, (1, 1), ((0, 0), (1, 1)), dimens...]
    unnamed x12 -> x11, local copies, waits for them, and re-layouts: 2.27 us -> 5.48 us
  transfers between devices with their start and end apart: 8 -> 0, of which waited for: 4 -> 0; matrix products, arithmetic and copies ran while one was open for 1% -> 0% of each run, Pallas kernels for 0% -> 0%
where the time goes in v1:
time: 42.6 us; the launch traced here: 42.4 us
  Pallas kernels  36.9 us (87%)
  local copies, waits for them, and re-layouts  5.48 us (13%)
    pallas_call x1, Pallas kernels, on_device(): pl.pallas_call(functools.partial(kernel, imgs, strips, height, cols), out...  36.9 us
    unnamed x11, local copies, waits for them, and re-layouts  5.48 us

profile of v1, /device:TPU:0, one launch (start us, length us, event | category | flops | bytes accessed | tf_op | source)
XLA Modules:
  0.0 42.4 jit_solution(5554051463029668566)
XLA Ops:
  0.0 0.0 copy-start
  0.0 1.6 %copy-done = bf16[1,8,128,1024]{3,2,1,0:T(8,128)(2,1)S(1)} copy-done((bf16[1,8,128,1024]{3,2,1,0:T(8,128)(2,1)S(1)}, bf16[1,8,128,1024]{3,2,1,0:T(8,128)(2,1)}, u32[]{:S(2)}) %copy-start) | copy-done | bytes 2097176
  1.6 0.0 copy-start.1
  1.6 1.0 %copy-done.1 = bf16[1024,256]{1,0:T(8,128)(2,1)S(1)} copy-done((bf16[1024,256]{1,0:T(8,128)(2,1)S(1)}, bf16[1024,256]{1,0:T(8,128)(2,1)}, u32[]{:S(2)}) %copy-start.1) | copy-done | bytes 524312
  2.6 0.0 copy-start.2
  2.6 0.7 %copy-done.2 = f32[4,256]{1,0:T(4,128)S(1)} copy-done((f32[4,256]{1,0:T(4,128)S(1)}, f32[4,256]{1,0:T(4,128)}, u32[]{:S(2)}) %copy-start.2) | copy-done | bytes 4120
  3.3 0.0 copy-start.3
  3.3 0.7 %copy-done.3 = f32[4,256]{1,0:T(4,128)S(1)} copy-done((f32[4,256]{1,0:T(4,128)S(1)}, f32[4,256]{1,0:T(4,128)}, u32[]{:S(2)}) %copy-start.3) | copy-done | bytes 4120
  4.0 0.0 copy-start.4
  4.0 0.7 %copy-done.4 = f32[256]{0:T(256)S(1)} copy-done((f32[256]{0:T(256)S(1)}, f32[256]{0:T(256)}, u32[]{:S(2)}) %copy-start.4) | copy-done | bytes 1048
  4.7 36.9 %shard_map.64 = bf16[1024,256]{1,0:T(8,128)(2,1)S(1)} custom-call(bf16[1024,1024]{1,0:T(8,128)(2,1)S(1)} %bitcast.4, bf16[1024,256]{1,0:T(8,128)(2,1)S(1)} %copy-done.1, f32[1,256]{1,0:T(1,128)S(1)} %bitcast.6, bf16[12,768,256]{2,1,0:T(8,128)(2,1)} %bitcast.7, f32[4,256]{1,0:T(4,128)S(1)} %copy-done.2, f32[4,256]{1,0:T(4,128)S(1)} %copy-done.3), custom_call_target="tpu_custom_call" | custom-call | tf_op jit(solution)/shard_map/pallas_call | solution.py:303
  41.6 0.8 %copy.8 = bf16[1,8,128,256]{3,2,1,0:T(8,128)(2,1)} copy(bf16[1,8,128,256]{3,2,1,0:T(8,128)(2,1)S(1)} %bitcast.5) | data formatting | bytes 1048576
Async XLA Ops:
  0.0 1.6 %copy-start = (bf16[1,8,128,1024]{3,2,1,0:T(8,128)(2,1)S(1)}, bf16[1,8,128,1024]{3,2,1,0:T(8,128)(2,1)}, u32[]{:S(2)}) copy-start(bf16[1,8,128,1024]{3,2,1,0:T(8,128)(2,1)} %param.6) | copy-start | bytes 6291460
  1.6 1.0 %copy-start.1 = (bf16[1024,256]{1,0:T(8,128)(2,1)S(1)}, bf16[1024,256]{1,0:T(8,128)(2,1)}, u32[]{:S(2)}) copy-start(bf16[1024,256]{1,0:T(8,128)(2,1)} %pw_ref.1) | copy-start | bytes 1572868
  2.6 0.7 %copy-start.2 = (f32[4,256]{1,0:T(4,128)S(1)}, f32[4,256]{1,0:T(4,128)}, u32[]{:S(2)}) copy-start(f32[4,256]{1,0:T(4,128)} %gain_ref.1) | copy-start | bytes 12292
  3.3 0.7 %copy-start.3 = (f32[4,256]{1,0:T(4,128)S(1)}, f32[4,256]{1,0:T(4,128)}, u32[]{:S(2)}) copy-start(f32[4,256]{1,0:T(4,128)} %bias_ref.1) | copy-start | bytes 12292
  4.0 0.7 %copy-start.4 = (f32[256]{0:T(256)S(1)}, f32[256]{0:T(256)}, u32[]{:S(2)}) copy-start(f32[256]{0:T(256)} %param.8) | copy-start | bytes 3076

commit v2 on v1

--- a/solution.py
+++ b/solution.py
@@ -11,6 +11,10 @@
 MESH = pl.DeviceIdType.MESH
 F32 = jnp.float32
 BF16 = jnp.bfloat16
+PLAN = ("flat",)
+UNROLL = 0
+ROWS = 2
+VMEM_LIMIT = 62 * 1024 * 1024
 
 
 def kernel(
@@ -32,7 +36,7 @@
     joined,
     xcat,
     raw,
-    stat,
+    stats,
     peers,
     load_sem,
     weight_sem,
@@ -52,6 +56,24 @@
         target = lax.rem(me + distance, count)
         return {"img": target // strips, "row": lax.rem(target, strips)}
 
+    def row_peer(distance):
+        return {"img": me_img, "row": lax.rem(me_row + distance, strips)}
+
+    def img_peer(distance):
+        return {"img": lax.rem(me_img + distance, imgs), "row": me_row}
+
+    def core_peer(distance):
+        return {"img": me_img, "row": me_row + 1 - 2 * lax.rem(me_row, 2)}
+
+    def chip_peer(distance):
+        chips = strips // 2
+        target = lax.rem(me_img * chips + me_row // 2 + distance, imgs * chips)
+        return {"img": target // chips, "row": 2 * lax.rem(target, chips) + lax.rem(me_row, 2)}
+
+    peer_of = {
+        "flat": peer, "row": row_peer, "img": img_peer, "core": core_peer, "chip": chip_peer
+    }
+
     def rows(first, number):
         return pl.ds(first * cols, number * cols)
 
@@ -165,51 +187,74 @@
         def _():
             down.wait_send()
 
+    def taps(k, first, number, which):
+        return sum(
+            jnp.dot(xcat[rows(first + dy, number), :], cw[3 * k + dy], preferred_element_type=F32)
+            for dy in which
+        )
+
+    def moments(value):
+        size = value.shape[0]
+        first = jnp.sum(value, axis=0, keepdims=True)
+        squares = jnp.sum(jnp.square(value - first / size), axis=0, keepdims=True)
+        return first, squares, size
+
     def conv(k, first, number):
-        total = None
-        for dy in range(3):
-            part = jnp.dot(
-                xcat[rows(first + dy, number), :], cw[3 * k + dy], preferred_element_type=F32
-            )
-            total = part if total is None else total + part
-        raw[k, rows(first + 1, number), :] = total
-        return jnp.sum(total, axis=0, keepdims=True)
-
-    def stat_copy(k, distance):
+        value = taps(k, first, number, range(3))
+        raw[k, rows(first + 1, number), :] = value
+        return moments(value)
+
+    def finish(k, first, dy):
+        value = raw[k, rows(first + 1, 1), :] + taps(k, first, 1, (dy,))
+        raw[k, rows(first + 1, 1), :] = value
+        return moments(value)
+
+    def stat_copy(k, stage, distance):
         return pltpu.make_async_remote_copy(
-            src_ref=stat.at[k],
-            dst_ref=peers.at[k, distance - 1],
-            send_sem=stat_send.at[k],
-            recv_sem=stat_recv.at[k],
-            device_id=peer(distance),
+            src_ref=stats[stage].at[k],
+            dst_ref=peers[stage].at[k, distance - 1],
+            send_sem=stat_send.at[k, stage],
+            recv_sem=stat_recv.at[k, stage],
+            device_id=peer_of[PLAN[stage]](distance),
             device_id_type=MESH,
         )
 
-    def send_stat(k, sums):
-        centre = sums / cells
-
-        def add_row(row, squares):
-            return squares + jnp.sum(
-                jnp.square(raw[k, span(row + 1), :] - centre), axis=0, keepdims=True
-            )
-
-        squares = lax.fori_loop(0, height, add_row, jnp.zeros((1, width), F32))
-        stat[k] = jnp.concatenate([sums, squares], axis=0)
-
-        @pl.loop(1, count)
-        def _(distance):
-            stat_copy(k, distance).start()
+    def spread_stat(k, stage):
+        others = peers[stage].shape[1]
+        if others <= UNROLL:
+            for distance in range(1, others + 1):
+                stat_copy(k, stage, distance).start()
+        else:
+            pl.loop(1, others + 1)(lambda distance: stat_copy(k, stage, distance).start())
+
+    def send_stat(k, chunks):
+        total = sum(chunk[0] for chunk in chunks)
+        centre = total / cells
+        squares = sum(
+            chunk[1] + jnp.square(chunk[0] / chunk[2] - centre) * chunk[2] for chunk in chunks
+        )
+        stats[0][k] = jnp.concatenate([total, squares], axis=0)
+        spread_stat(k, 0)
 
     def take_stat(k):
-        pltpu.make_async_copy(peers.at[k], peers.at[k], stat_recv.at[k]).wait()
-        own = stat[k]
-        every = peers[k]
-        total = jnp.sum(every, axis=0) + own
-        average = total[0:1] / (count * cells)
-        gaps = jnp.sum(jnp.square(every[:, 0, :] - cells * average), axis=0, keepdims=True)
-        gaps += jnp.square(own[0:1] - cells * average)
-        spread = (total[1:2] + gaps / cells) / (count * cells)
-        scale = lax.rsqrt(spread + epsilon) * gain_ref[pl.ds(k, 1), :]
+        size = cells
+        for stage in range(len(PLAN)):
+            buffer = peers[stage]
+            others = buffer.shape[1]
+            own = stats[stage][k]
+            pltpu.make_async_copy(buffer.at[k], buffer.at[k], stat_recv.at[k, stage]).wait()
+            every = buffer[k]
+            total = jnp.sum(every, axis=0) + own
+            even = total[0:1] / (others + 1)
+            gaps = jnp.sum(jnp.square(every[:, 0, :] - even), axis=0, keepdims=True)
+            gaps += jnp.square(own[0:1] - even)
+            squares = total[1:2] + gaps / size
+            size *= others + 1
+            if stage + 1 < len(PLAN):
+                stats[stage + 1][k] = jnp.concatenate([total[0:1], squares], axis=0)
+                spread_stat(k, stage + 1)
+        average = total[0:1] / size
+        scale = lax.rsqrt(squares / size + epsilon) * gain_ref[pl.ds(k, 1), :]
         return average, scale, bias_ref[pl.ds(k, 1), :]
 
     def normed(k, row, norm):
@@ -218,6 +263,7 @@
 
     rim_first = [(0, 2), (height - 2, 2)]
     middle = [(first, 2) for first in range(2, height - 2, 2)]
+    inside = [(first, 2) for first in range(1, height - 1, 2)]
 
     loads[0].wait()
     loads[1].wait()
@@ -228,7 +274,7 @@
     send_halo(feat, 0)
     loads[3].wait()
 
-    @pl.loop(1, height - 1)
+    @pl.loop(1, height - 1, unroll=ROWS)
     def _(row):
         project(row)
 
@@ -236,19 +282,21 @@
         put(row, jnp.maximum(feat[span(row), :].astype(F32), 0.0))
 
     weights[0].wait()
-    sums = sum(conv(0, first, number) for first, number in middle)
+    chunks = [conv(0, first, number) for first, number in inside]
+    raw[0, rows(1, 1), :] = taps(0, 0, 1, (1, 2))
+    raw[0, rows(height, 1), :] = taps(0, height - 1, 1, (0, 1))
     take_halo(feat, 0, lambda: feature_rim(0), lambda: feature_rim(height + 1))
-    sums += sum(conv(0, first, number) for first, number in rim_first)
+    chunks += [finish(0, 0, 0), finish(0, height - 1, 2)]
     send_halo(raw.at[0], 1)
-    send_stat(0, sums)
+    send_stat(0, chunks)
 
     def later_conv(k):
         weights[k].wait()
-        sums = sum(conv(k, first, number) for first, number in rim_first)
+        chunks = [conv(k, first, number) for first, number in rim_first]
         if k < 3:
             send_halo(raw.at[k], k + 1)
-        sums += sum(conv(k, first, number) for first, number in middle)
-        send_stat(k, sums)
+        chunks += [conv(k, first, number) for first, number in middle]
+        send_stat(k, chunks)
 
     def hidden(k):
         norm = take_stat(k)
@@ -256,7 +304,7 @@
         def one(row):
             put(row, jnp.maximum(normed(k, row, norm), 0.0))
 
-        pl.loop(1, height + 1)(one)
+        pl.loop(1, height + 1, unroll=ROWS)(one)
         take_halo(raw.at[k], k + 1, lambda: one(0), lambda: one(height + 1))
 
     hidden(0)
@@ -270,14 +318,14 @@
             joined[span(row - 1), :] = value
         put(row, jnp.maximum(value.astype(F32), 0.0))
 
-    pl.loop(1, height + 1)(lambda row: join(row, True))
+    pl.loop(1, height + 1, unroll=ROWS)(lambda row: join(row, True))
     take_halo(raw.at[1], 2, lambda: join(0, False), lambda: join(height + 1, False))
     later_conv(2)
     hidden(2)
     later_conv(3)
     norm_3 = take_stat(3)
 
-    @pl.loop(0, height)
+    @pl.loop(0, height, unroll=ROWS)
     def _(row):
         value = joined[span(row), :].astype(F32) + normed(3, row + 1, norm_3)
         out_ref[span(row), :] = value.astype(BF16)
@@ -286,7 +334,8 @@
     for k in range(3):
         end_halo(raw.at[k], k + 1)
     for k in range(4):
-        pltpu.make_async_copy(peers.at[k], peers.at[k], stat_send.at[k]).wait()
+        for stage, buffer in enumerate(peers):
+            pltpu.make_async_copy(buffer.at[k], buffer.at[k], stat_send.at[k, stage]).wait()
 
 
 def solution(mesh):
@@ -297,8 +346,9 @@
         convs, taps, _, width, _ = conv_weight.shape
         assert images == 1 and height % 2 == 0 and height >= 4
         count = imgs * strips
+        sizes = {"flat": count, "row": strips, "img": imgs, "core": 2, "chip": count // 2}
         cells = height * cols
-        any_space = pl.BlockSpec(memory_space=pl.ANY)
+        any_space = pl.BlockSpec(memory_space=pltpu.HBM)
         vmem = pl.BlockSpec(memory_space=pltpu.VMEM)
         out = pl.pallas_call(
             functools.partial(kernel, imgs, strips, height, cols),
@@ -313,17 +363,17 @@
                 pltpu.VMEM((cells, width), BF16),
                 pltpu.VMEM((cells + 2 * cols, taps * width), BF16),
                 pltpu.VMEM((convs, cells + 2 * cols, width), F32),
-                pltpu.VMEM((convs, 2, width), F32),
-                pltpu.VMEM((convs, count - 1, 2, width), F32),
+                [pltpu.VMEM((convs, 2, width), F32) for _ in PLAN],
+                [pltpu.VMEM((convs, sizes[part] - 1, 2, width), F32) for part in PLAN],
                 pltpu.SemaphoreType.DMA((4,)),
                 pltpu.SemaphoreType.DMA((convs,)),
                 pltpu.SemaphoreType.DMA((convs, 2)),
                 pltpu.SemaphoreType.DMA((convs, 2)),
-                pltpu.SemaphoreType.DMA((convs,)),
-                pltpu.SemaphoreType.DMA((convs,)),
+                pltpu.SemaphoreType.DMA((convs, len(PLAN))),
+                pltpu.SemaphoreType.DMA((convs, len(PLAN))),
             ],
             compiler_params=pltpu.CompilerParams(
-                collective_id=0, has_side_effects=True, vmem_limit_bytes=48 * 1024 * 1024
+                collective_id=0, has_side_effects=True, vmem_limit_bytes=VMEM_LIMIT
             ),
         )(
             tokens.reshape(cells, embed),

time: 42.6 us -> 39.3 us (0.923)
  local copies, waits for them, and re-layouts: 5.48 us -> 1.87 us
    unnamed x11 -> x1, local copies, waits for them, and re-layouts: 5.48 us -> 1.87 us
where the time goes in v2:
time: 39.3 us; the launch traced here: 39.1 us
  Pallas kernels  37.2 us (95%)
  local copies, waits for them, and re-layouts  1.87 us (5%)
    pallas_call x1, Pallas kernels, on_device(): pl.pallas_call(functools.partial(kernel, imgs, strips, height, cols), out...  37.2 us
    unnamed x1, local copies, waits for them, and re-layouts  1.87 us

profile of v2, /device:TPU:0, one launch (start us, length us, event | category | flops | bytes accessed | tf_op | source)
XLA Modules:
  0.0 39.1 jit_solution(4419550940015387843)
XLA Ops:
  0.0 37.2 %shard_map.64 = bf16[1024,256]{1,0:T(8,128)(2,1)} custom-call(bf16[1024,1024]{1,0:T(8,128)(2,1)} %bitcast.5, bf16[1024,256]{1,0:T(8,128)(2,1)} %pw_ref.1, f32[1,256]{1,0:T(1,128)} %bitcast.7, bf16[12,768,256]{2,1,0:T(8,128)(2,1)} %bitcast.4, f32[4,256]{1,0:T(4,128)} %gain_ref.1, f32[4,256]{1,0:T(4,128)} %bias_ref.1), custom_call_target="tpu_custom_call" | custom-call | tf_op jit(solution)/shard_map/pallas_call | solution.py:353
  37.2 1.9 %copy.8 = bf16[1,8,128,256]{3,2,1,0:T(8,128)(2,1)} copy(bf16[1,8,128,256]{3,2,1,0:T(8,128)(2,1)} %bitcast.6) | data formatting | bytes 1048576
